TPU v7x, 128 devices: a whole 4x4x4 slice. The times are simulated.
128 devices in a mesh: gx: 4 (over x), gy: 32 (over z, y, core).
Axes of the slice: x: 4, y: 4, z: 4, core: 2. Of those that a mesh axis runs over, the one named last changes fastest.
Arguments:
- schur_blocks: float32 [128, 2048, 2048], P(('gx', 'gy')), may hold values from -1 to 11, as said below
- offsets: int32 [128], P(('gx', 'gy')), may hold values from 256 to 768, as said below
- right_side: float32 [131072, 128], P(('gx', 'gy')), may hold values from -20 to 20
- coarse_basis: float32 [131072, 128], P(('gx', 'gy')), may hold values from -0.015625 to 0.015625
- coarse_load: float32 [128, 128], replicated, may hold values from -6 to 6
Outputs:
- multipliers: float32 [131072, 128], P(('gx', 'gy'))
- amplitudes: float32 [128, 128], replicated
Inputs may be any that keep to these rules, and one draw needn't show every extreme that they name: `schur_blocks`: each block is symmetric positive definite. `offsets`: both ends of the range are taken by some subdomain.
All inputs are finite; a program needn't handle non-finite values.
Results may differ from a plain program's by a relative error of at most 0.0003.
Values sent between devices are 32-bit elements; how exact they have to be, the bound alone decides.
A program may use at most 128 MiB of HBM per device.

v0:
```python
import jax
import jax.numpy as jnp
from jax import lax
from jax.sharding import Mesh
from jax.sharding import PartitionSpec as P

ITERS = 3
GX_GY = ("gx", "gy_0", "gy_1", "gy_2")


HIGHEST = lax.Precision.HIGHEST


def extended_2(shard, sides, width):
    edges = {}
    for axis, dim in sides:
        peers, length = (lax.axis_size(axis), shard.shape[dim])
        up = [(i, (i + 1) % peers) for i in range(peers - 1)]
        last = lax.slice_in_dim(shard, length - width, length, axis=dim)
        initial = lax.slice_in_dim(shard, 0, width, axis=dim)
        edges[dim] = (
            lax.ppermute(last, axis, up),
            lax.ppermute(initial, axis, [(b, a) for a, b in up]),
        )
    done = []
    for _, dim in sides:
        low, high = edges[dim]
        around = [(width, width) if d in done else (0, 0) for d in range(shard.ndim)]
        shard = jnp.concatenate([jnp.pad(low, around), shard, jnp.pad(high, around)], axis=dim)
        done.append(dim)
    return shard


def cut_along(shard, dim, peers):
    shape = shard.shape
    pieces = shard.reshape(*shape[:dim], peers, shape[dim] // peers, *shape[dim + 1 :])
    return jnp.moveaxis(pieces, dim, 0)


def sum_at_owner(shard, axis, dim):
    peers = lax.axis_size(axis)
    pieces = lax.all_to_all(cut_along(shard, dim, peers), axis, 0, 0, tiled=True)
    return jnp.sum(pieces, axis=0)


def sum_in_two_steps(shard, axes, dim):
    far, near = axes
    own = sum_at_owner(cut_along(shard, dim, lax.axis_size(far)), near, dim + 1)
    return jnp.sum(lax.all_to_all(own, far, 0, 0, tiled=True), axis=0)


def filled_up(lines, peers):
    spare = -lines.shape[0] % peers
    if not spare:
        return lines
    return jnp.concatenate([lines, jnp.zeros((spare, *lines.shape[1:]), lines.dtype)])


def sent_to_all(shard, axis):
    copies = jnp.broadcast_to(shard, (lax.axis_size(axis), *shard.shape))
    return lax.all_to_all(copies, axis, split_axis=0, concat_axis=0, tiled=True)


def in_order(pieces, dim):
    shape = list(pieces.shape[1:])
    shape[dim] *= pieces.shape[0]
    return jnp.moveaxis(pieces, 0, dim).reshape(shape)


def gathered_by_axis(shard, axes, dim):
    far, near = axes
    initial = sent_to_all(shard, far)
    pieces = jnp.swapaxes(sent_to_all(initial, near), 0, 1)
    return in_order(pieces.reshape(-1, *shard.shape), dim)


def nested_sum(shard, axes):
    lines = shard.reshape(-1, shard.shape[-1])
    own = sum_in_two_steps(
        filled_up(lines, lax.axis_size(axes[0]) * lax.axis_size(axes[1])), axes, 0
    )
    whole = gathered_by_axis(own, axes, 0)
    return whole[: len(lines)].reshape(shard.shape)


def taken_together(shard, axis):
    everything = sent_to_all(shard, axis)
    return jnp.sum(everything, axis=0)


def over_axes(shard, axes):
    far, near = axes
    nearer = taken_together(shard, near)
    return taken_together(nearer, far)


def apply_local(vector, schur_block, start_row):
    slab_rows = vector.shape[0]
    window_rows = schur_block.shape[0]
    reach_rows = 3 * slab_rows // 4
    skip_rows = slab_rows - reach_rows
    extended = extended_2(vector, ((GX_GY, 0),), reach_rows)
    first_row = start_row - skip_rows
    window = lax.dynamic_slice_in_dim(extended, first_row, window_rows, 0)
    product_block = jnp.dot(
        schur_block, window, precision=HIGHEST, preferred_element_type=jnp.float32
    )
    spread = jnp.zeros((3 * slab_rows, vector.shape[1]), jnp.float32)
    spread = lax.dynamic_update_slice_in_dim(spread, product_block, start_row, 0)
    to_left = spread[:slab_rows]
    own_part = spread[slab_rows : 2 * slab_rows]
    to_right = spread[2 * slab_rows :]
    packed = jnp.concatenate([to_left, to_right], axis=0)
    arrived = extended_2(packed, ((GX_GY, 0),), slab_rows)
    result = own_part + arrived[:slab_rows] + arrived[3 * slab_rows :]
    return result


def project_sum(residual, coarse_basis, gram_factor):
    local_coarse = jnp.dot(
        coarse_basis.T, residual, precision=HIGHEST, preferred_element_type=jnp.float32
    )
    coarse_part = nested_sum(local_coarse, (("gx", "gy_0", "gy_1"), "gy_2"))
    amplitudes = jax.scipy.linalg.cho_solve((gram_factor, True), coarse_part)
    projected = residual - jnp.dot(
        coarse_basis, amplitudes, precision=HIGHEST, preferred_element_type=jnp.float32
    )
    energy = over_axes(jnp.sum(projected * projected, axis=0), (("gx", "gy_0", "gy_1"), "gy_2"))
    return (projected, amplitudes, energy)


def local(schur_blocks, offsets, right_side, coarse_basis, coarse_load):
    schur_block = schur_blocks[0]
    start_row = offsets[0]
    local_gram = jnp.dot(
        coarse_basis.T, coarse_basis, precision=HIGHEST, preferred_element_type=jnp.float32
    )
    gram_matrix = nested_sum(local_gram, (("gx", "gy_0", "gy_1"), "gy_2"))
    gram_factor = jnp.linalg.cholesky(gram_matrix)
    start_load = jax.scipy.linalg.cho_solve((gram_factor, True), coarse_load)
    multipliers = jnp.dot(
        coarse_basis, start_load, precision=HIGHEST, preferred_element_type=jnp.float32
    )
    residual = right_side - apply_local(multipliers, schur_block, start_row)
    projected, amplitudes, energy_now = project_sum(residual, coarse_basis, gram_factor)
    direction = projected
    for iteration in range(ITERS):
        operator_image = apply_local(direction, schur_block, start_row)
        curvature = over_axes(
            jnp.sum(direction * operator_image, axis=0), (("gx", "gy_0", "gy_1"), "gy_2")
        )
        step_length = energy_now / curvature
        multipliers = multipliers + step_length * direction
        residual = residual - step_length * operator_image
        projected, amplitudes, energy_next = project_sum(residual, coarse_basis, gram_factor)
        direction = projected + energy_next / energy_now * direction
        energy_now = energy_next
    return (multipliers, amplitudes)


def solution(mesh):
    split = Mesh(mesh.devices.reshape(mesh.shape["gx"], 4, 4, 2), ("gx", "gy_0", "gy_1", "gy_2"))
    in_specs = (P(GX_GY, None, None), P(GX_GY), P(GX_GY, None), P(GX_GY, None), P())
    out_specs = (P(GX_GY, None), P())
    return jax.shard_map(local, mesh=split, in_specs=in_specs, out_specs=out_specs, check_vma=False)
```

profile of v0, /device:TPU:1, one launch (start us, length us, event | category | flops | bytes accessed | tf_op | source)
XLA Modules:
  0.0 608.6 jit_solution(10132944279101455514)
XLA Ops:
  9.1 19.5 %all_to_all.203 = f32[64,1,128]{2,1,0:T(1,128)S(1)} all-to-all(f32[64,1,128]{2,1,0:T(1,128)S(1)} %bitcast.188), channel_id=1, replica_groups=mesh['gx'=4,'gy_0'=4,'gy_1'=4,'gy_2'=2] {'gx','gy_0','gy_1'}, dimensions={0} | all-to-all | bytes 65536 | tf_op jit(solution)/shard_map/all_to_all | solution.py:49
  28.6 12.9 %all_to_all.187 = f32[64,1,128]{2,1,0:T(1,128)S(1)} all-to-all(f32[64,1,128]{2,1,0:T(1,128)S(1)} %broadcast_in_dim.76), channel_id=1, replica_groups=mesh['gx'=4,'gy_0'=4,'gy_1'=4,'gy_2'=2] {'gx','gy_0','gy_1'}, dimensions={0} | all-to-all | bytes 65536 | tf_op jit(solution)/shard_map/all_to_all | solution.py:61
  41.6 6.6 %all_to_all.188 = f32[2,64,1,128]{3,1,2,0:T(8,128)S(1)} all-to-all(f32[2,64,1,128]{3,1,2,0:T(8,128)S(1)} %broadcast_in_dim.77), channel_id=1, replica_groups=mesh['gx'=4,'gy_0'=4,'gy_1'=4,'gy_2'=2] {'gy_2'}, dimensions={0} | all-to-all | bytes 131072 | tf_op jit(solution)/shard_map/all_to_all | solution.py:61
  48.4 11.7 %cholesky.18 = f32[128,128]{1,0:T(8,128)S(1)} custom-call(f32[128,128]{1,0:T(8,128)S(1)} %fusion.65), custom_call_target="Cholesky" | custom-call | tf_op jit(solution)/shard_map/jit(cholesky)/cholesky | solution.py:139
  61.4 9.8 %custom-call.12 = f32[1,128,128]{1,2,0:T(8,128)S(1)} custom-call(f32[1,128,128]{2,1,0:T(8,128)S(1)} %fusion.44), custom_call_target="InvertDiagBlocksLowerTriangular" | custom-call | tf_op jit(solution)/shard_map/jit(_cho_solve)/triangular_solve | solution.py:140
  84.0 20.9 %fusion.8 = f32[2048,128]{0,1:T(8,128)} fusion(f32[1,2048,2048]{2,1,0:T(8,128)} %param.7, s32[]{:T(128)S(6)} %select_n.9, f32[768,128]{0,1:T(8,128)S(1)} %collective-permute-done, f32[1024,128]{0,1:T(8,128)S(1)} %convolution_bitcast_fusion.3, f32[768,128]{0,1:T(8,128)S(1)} %collective-permute-done.1), kind=kOutput, calls=%fused_computation.8 | convolution fusion | flops 6442975232 | bytes 19136516 | tf_op jit(solution)/shard_map/dot_general | solution.py:105
  105.1 5.3 dynamic_update_slice.12
  130.4 24.7 %all_to_all.204 = f32[64,1,128]{2,1,0:T(1,128)S(1)} all-to-all(f32[64,1,128]{2,1,0:T(1,128)S(1)} %bitcast.190), channel_id=1, replica_groups=mesh['gx'=4,'gy_0'=4,'gy_1'=4,'gy_2'=2] {'gx','gy_0','gy_1'}, dimensions={0} | all-to-all | bytes 65536 | tf_op jit(solution)/shard_map/all_to_all | solution.py:49
  155.2 12.9 %all_to_all.190 = f32[64,1,128]{2,1,0:T(1,128)S(1)} all-to-all(f32[64,1,128]{2,1,0:T(1,128)S(1)} %broadcast_in_dim.78), channel_id=1, replica_groups=mesh['gx'=4,'gy_0'=4,'gy_1'=4,'gy_2'=2] {'gx','gy_0','gy_1'}, dimensions={0} | all-to-all | bytes 65536 | tf_op jit(solution)/shard_map/all_to_all | solution.py:61
  168.1 6.6 %all_to_all.191 = f32[2,64,1,128]{3,1,2,0:T(8,128)S(1)} all-to-all(f32[2,64,1,128]{3,1,2,0:T(8,128)S(1)} %broadcast_in_dim.79), channel_id=1, replica_groups=mesh['gx'=4,'gy_0'=4,'gy_1'=4,'gy_2'=2] {'gy_2'}, dimensions={0} | all-to-all | bytes 131072 | tf_op jit(solution)/shard_map/all_to_all | solution.py:61
  187.6 20.9 %fusion.11 = f32[2048,128]{0,1:T(8,128)} fusion(f32[1,2048,2048]{2,1,0:T(8,128)} %param.7, s32[]{:T(128)S(6)} %select_n.9, f32[768,128]{0,1:T(8,128)S(1)} %collective-permute-done.4, f32[1024,128]{0,1:T(8,128)S(1)} %fusion.20, f32[768,128]{0,1:T(8,128)S(1)} %collective-permute-done.5), kind=kOutput, calls=%fused_computation.9 | convolution fusion | flops 6442975232 | bytes 19136516 | tf_op jit(solution)/shard_map/dot_general | solution.py:105
  236.4 16.5 %all-to-all-start.9 = ((f32[64,1,128]{2,1,0:T(1,128)}), f32[64,1,128]{2,1,0:T(1,128)S(1)}, u32[]{:S(2)}, u32[]{:S(2)}) async-start(f32[64,1,128]{2,1,0:T(1,128)} %broadcast_in_dim.81), calls=%async_computation.9 | async-start | bytes 65536 | tf_op jit(solution)/shard_map/all_to_all | solution.py:61
  252.9 8.3 %all-to-all-done.9 = f32[64,1,128]{2,1,0:T(1,128)S(1)} async-done(((f32[64,1,128]{2,1,0:T(1,128)}), f32[64,1,128]{2,1,0:T(1,128)S(1)}, u32[]{:S(2)}, u32[]{:S(2)}) %all-to-all-start.9) | async-done | bytes 32800 | tf_op jit(solution)/shard_map/all_to_all | solution.py:61
  266.6 8.3 %all-to-all-done.11 = f32[64,1,128]{2,1,0:T(1,128)S(1)} async-done(((f32[64,1,128]{2,1,0:T(1,128)}), f32[64,1,128]{2,1,0:T(1,128)S(1)}, u32[]{:S(2)}, u32[]{:S(2)}) %all-to-all-start.11) | async-done | bytes 32800 | tf_op jit(solution)/shard_map/all_to_all | solution.py:61
  278.3 6.8 %all_to_all.193 = f32[2,64,1,128]{3,1,2,0:T(8,128)S(1)} all-to-all(f32[2,64,1,128]{3,1,2,0:T(8,128)S(1)} %bitcast.181), channel_id=1, replica_groups=mesh['gx'=4,'gy_0'=4,'gy_1'=4,'gy_2'=2] {'gy_2'}, dimensions={0} | all-to-all | bytes 131072 | tf_op jit(solution)/shard_map/all_to_all | solution.py:42
  285.0 12.9 %all_to_all.205 = f32[64,1,128]{2,1,0:T(1,128)S(1)} all-to-all(f32[64,1,128]{2,1,0:T(1,128)S(1)} %bitcast.192), channel_id=1, replica_groups=mesh['gx'=4,'gy_0'=4,'gy_1'=4,'gy_2'=2] {'gx','gy_0','gy_1'}, dimensions={0} | all-to-all | bytes 65536 | tf_op jit(solution)/shard_map/all_to_all | solution.py:49
  298.0 12.9 %all_to_all.206 = f32[64,1,128]{2,1,0:T(1,128)S(1)} all-to-all(f32[64,1,128]{2,1,0:T(1,128)S(1)} %broadcast_in_dim.84), channel_id=1, replica_groups=mesh['gx'=4,'gy_0'=4,'gy_1'=4,'gy_2'=2] {'gx','gy_0','gy_1'}, dimensions={0} | all-to-all | bytes 65536 | tf_op jit(solution)/shard_map/all_to_all | solution.py:61
  311.0 6.6 %all_to_all.194 = f32[2,64,1,128]{3,1,2,0:T(8,128)S(1)} all-to-all(f32[2,64,1,128]{3,1,2,0:T(8,128)S(1)} %broadcast_in_dim.85), channel_id=1, replica_groups=mesh['gx'=4,'gy_0'=4,'gy_1'=4,'gy_2'=2] {'gy_2'}, dimensions={0} | all-to-all | bytes 131072 | tf_op jit(solution)/shard_map/all_to_all | solution.py:61
  322.7 12.9 %all_to_all.207 = f32[64,1,128]{2,1,0:T(1,128)S(1)} all-to-all(f32[64,1,128]{2,1,0:T(1,128)S(1)} %broadcast_in_dim.87), channel_id=1, replica_groups=mesh['gx'=4,'gy_0'=4,'gy_1'=4,'gy_2'=2] {'gx','gy_0','gy_1'}, dimensions={0} | all-to-all | bytes 65536 | tf_op jit(solution)/shard_map/all_to_all | solution.py:61
  348.8 20.9 %fusion.14 = f32[2048,128]{0,1:T(8,128)} fusion(f32[1,2048,2048]{2,1,0:T(8,128)} %param.7, s32[]{:T(128)S(6)} %select_n.9, f32[768,128]{0,1:T(8,128)S(1)} %collective-permute-done.8, f32[1024,128]{0,1:T(8,128)S(1)} %multiply_add_fusion.2, f32[768,128]{0,1:T(8,128)S(1)} %collective-permute-done.9), kind=kOutput, calls=%fused_computation.10 | convolution fusion | flops 6442975232 | bytes 19136516 | tf_op jit(solution)/shard_map/dot_general | solution.py:105
  370.9 6.2 %dynamic_update_slice.14 = f32[3072,128]{0,1:T(8,128)} dynamic-update-slice(f32[3072,128]{0,1:T(8,128)} %broadcast.113.clone.2, f32[2048,128]{0,1:T(8,128)} %fusion.14, s32[]{:T(128)S(6)} %select_n.18, s32[]{:T(128)} %constant.55.clone.1) | dynamic-update-slice | bytes 2097156 | tf_op jit(solution)/shard_map/dynamic_update_slice | solution.py:109
  396.3 24.8 %all_to_all.208 = f32[64,1,128]{2,1,0:T(1,128)S(1)} all-to-all(f32[64,1,128]{2,1,0:T(1,128)S(1)} %broadcast_in_dim.89), channel_id=1, replica_groups=mesh['gx'=4,'gy_0'=4,'gy_1'=4,'gy_2'=2] {'gx','gy_0','gy_1'}, dimensions={0} | all-to-all | bytes 65536 | tf_op jit(solution)/shard_map/all_to_all | solution.py:61
  428.8 12.9 %all_to_all.209 = f32[64,1,128]{2,1,0:T(1,128)S(1)} all-to-all(f32[64,1,128]{2,1,0:T(1,128)S(1)} %bitcast.194), channel_id=1, replica_groups=mesh['gx'=4,'gy_0'=4,'gy_1'=4,'gy_2'=2] {'gx','gy_0','gy_1'}, dimensions={0} | all-to-all | bytes 65536 | tf_op jit(solution)/shard_map/all_to_all | solution.py:49
  441.8 12.9 %all_to_all.210 = f32[64,1,128]{2,1,0:T(1,128)S(1)} all-to-all(f32[64,1,128]{2,1,0:T(1,128)S(1)} %broadcast_in_dim.90), channel_id=1, replica_groups=mesh['gx'=4,'gy_0'=4,'gy_1'=4,'gy_2'=2] {'gx','gy_0','gy_1'}, dimensions={0} | all-to-all | bytes 65536 | tf_op jit(solution)/shard_map/all_to_all | solution.py:61
  454.7 6.6 %all_to_all.198 = f32[2,64,1,128]{3,1,2,0:T(8,128)S(1)} all-to-all(f32[2,64,1,128]{3,1,2,0:T(8,128)S(1)} %broadcast_in_dim.91), channel_id=1, replica_groups=mesh['gx'=4,'gy_0'=4,'gy_1'=4,'gy_2'=2] {'gy_2'}, dimensions={0} | all-to-all | bytes 131072 | tf_op jit(solution)/shard_map/all_to_all | solution.py:61
  467.1 12.9 %all_to_all.211 = f32[64,1,128]{2,1,0:T(1,128)S(1)} all-to-all(f32[64,1,128]{2,1,0:T(1,128)S(1)} %broadcast_in_dim.93), channel_id=1, replica_groups=mesh['gx'=4,'gy_0'=4,'gy_1'=4,'gy_2'=2] {'gx','gy_0','gy_1'}, dimensions={0} | all-to-all | bytes 65536 | tf_op jit(solution)/shard_map/all_to_all | solution.py:61
  494.3 20.9 %fusion.17 = f32[2048,128]{0,1:T(8,128)} fusion(f32[1,2048,2048]{2,1,0:T(8,128)} %param.7, s32[]{:T(128)S(6)} %select_n.9, f32[768,128]{0,1:T(8,128)S(1)} %collective-permute-done.12, f32[1024,128]{0,1:T(8,128)S(1)} %multiply_add_fusion.1, f32[768,128]{0,1:T(8,128)S(1)} %collective-permute-done.13), kind=kOutput, calls=%fused_computation.11 | convolution fusion | flops 6442975232 | bytes 19136516 | tf_op jit(solution)/shard_map/dot_general | solution.py:105
  516.4 6.2 %dynamic_update_slice.15 = f32[3072,128]{0,1:T(8,128)} dynamic-update-slice(f32[3072,128]{0,1:T(8,128)} %broadcast.113, f32[2048,128]{0,1:T(8,128)} %fusion.17, s32[]{:T(128)S(6)} %select_n.18, s32[]{:T(128)} %constant.55.clone.1) | dynamic-update-slice | bytes 2097156 | tf_op jit(solution)/shard_map/dynamic_update_slice | solution.py:109
  541.2 24.8 %all_to_all.212 = f32[64,1,128]{2,1,0:T(1,128)S(1)} all-to-all(f32[64,1,128]{2,1,0:T(1,128)S(1)} %broadcast_in_dim.95), channel_id=1, replica_groups=mesh['gx'=4,'gy_0'=4,'gy_1'=4,'gy_2'=2] {'gx','gy_0','gy_1'}, dimensions={0} | all-to-all | bytes 65536 | tf_op jit(solution)/shard_map/all_to_all | solution.py:61
  573.6 12.9 %all_to_all.213 = f32[64,1,128]{2,1,0:T(1,128)S(1)} all-to-all(f32[64,1,128]{2,1,0:T(1,128)S(1)} %bitcast.196), channel_id=1, replica_groups=mesh['gx'=4,'gy_0'=4,'gy_1'=4,'gy_2'=2] {'gx','gy_0','gy_1'}, dimensions={0} | all-to-all | bytes 65536 | tf_op jit(solution)/shard_map/all_to_all | solution.py:49
  593.2 7.1 %all-to-all-done.30 = f32[64,1,128]{2,1,0:T(1,128)S(1)} async-done(((f32[64,1,128]{2,1,0:T(1,128)}), f32[64,1,128]{2,1,0:T(1,128)S(1)}, u32[]{:S(2)}, u32[]{:S(2)}) %all-to-all-start.30) | async-done | bytes 32800 | tf_op jit(solution)/shard_map/all_to_all | solution.py:61
  600.3 6.6 %all_to_all.202 = f32[2,64,1,128]{3,1,2,0:T(8,128)S(1)} all-to-all(f32[2,64,1,128]{3,1,2,0:T(8,128)S(1)} %broadcast_in_dim.97), channel_id=1, replica_groups=mesh['gx'=4,'gy_0'=4,'gy_1'=4,'gy_2'=2] {'gy_2'}, dimensions={0} | all-to-all | bytes 131072 | tf_op jit(solution)/shard_map/all_to_all | solution.py:61
  (177 shorter events, 193.4 us)
Async XLA Ops:
  0.6 1.0 copy-start
  0.6 70.6 %copy-start.11 = (f32[128,128]{1,0:T(8,128)S(1)}, f32[128,128]{1,0:T(8,128)}, u32[]{:S(2)}) copy-start(f32[128,128]{1,0:T(8,128)} %param.11) | copy-start | bytes 196612
  3.3 5.7 all-to-all-start
  72.5 7.1 %collective-permute-start = (f32[768,128]{0,1:T(8,128)S(1)}, f32[768,128]{0,1:T(8,128)S(1)}, u32[]{:S(2)}, u32[]{:S(2)}) collective-permute-start(f32[768,128]{0,1:T(8,128)S(1)} %get-tuple-element.30), channel_id=1, source_target_pairs={{0,1},{1,2},{2,3},{3,4},{4,5},{5,6},{6,7},{7,8},{8,9},{9,10},{10,1... | collective-permute-start | bytes 1179656 | tf_op jit(solution)/shard_map/ppermute | solution.py:22
  74.9 9.1 %collective-permute-start.1 = (f32[768,128]{0,1:T(8,128)S(1)}, f32[768,128]{0,1:T(8,128)S(1)}, u32[]{:S(2)}, u32[]{:S(2)}) collective-permute-start(f32[768,128]{0,1:T(8,128)S(1)} %get-tuple-element.29), channel_id=1, source_target_pairs={{1,0},{2,1},{3,2},{4,3},{5,4},{6,5},{7,6},{8,7},{9,8},{10,9},{11,1... | collective-permute-start | bytes 1179656 | tf_op jit(solution)/shard_map/ppermute | solution.py:23
  110.3 7.5 %copy-start.4 = (f32[3072,128]{0,1:T(8,128)}, f32[3072,128]{0,1:T(8,128)S(1)}, u32[]{:S(2)}) copy-start(f32[3072,128]{0,1:T(8,128)S(1)} %dynamic_update_slice.12) | copy-start | bytes 4718596
  111.5 8.5 %collective-permute-start.2 = (f32[1024,128]{0,1:T(8,128)}, f32[1024,128]{0,1:T(8,128)}, u32[]{:S(2)}, u32[]{:S(2)}) collective-permute-start(f32[1024,128]{0,1:T(8,128)} %get-tuple-element.21), channel_id=1, source_target_pairs={{0,1},{1,2},{2,3},{3,4},{4,5},{5,6},{6,7},{7,8},{8,9},{9,10},{10,1... | collective-permute-start | bytes 1572872 | tf_op jit(solution)/shard_map/ppermute | solution.py:22
  113.6 10.8 %collective-permute-start.3 = (f32[1024,128]{0,1:T(8,128)}, f32[1024,128]{0,1:T(8,128)}, u32[]{:S(2)}, u32[]{:S(2)}) collective-permute-start(f32[1024,128]{0,1:T(8,128)} %get-tuple-element.22), channel_id=1, source_target_pairs={{1,0},{2,1},{3,2},{4,3},{5,4},{6,5},{7,6},{8,7},{9,8},{10,9},{11,1... | collective-permute-start | bytes 1572872 | tf_op jit(solution)/shard_map/ppermute | solution.py:23
  125.9 50.1 %copy-start.1 = (f32[1024,128]{0,1:T(8,128)}, f32[1024,128]{0,1:T(8,128)S(1)}, u32[]{:S(2)}) copy-start(f32[1024,128]{0,1:T(8,128)S(1)} %fusion.39) | copy-start | bytes 1572868
  176.1 7.1 %collective-permute-start.4 = (f32[768,128]{0,1:T(8,128)S(1)}, f32[768,128]{0,1:T(8,128)S(1)}, u32[]{:S(2)}, u32[]{:S(2)}) collective-permute-start(f32[768,128]{0,1:T(8,128)S(1)} %get-tuple-element.28), channel_id=1, source_target_pairs={{0,1},{1,2},{2,3},{3,4},{4,5},{5,6},{6,7},{7,8},{8,9},{9,10},{10,1... | collective-permute-start | bytes 1179656 | tf_op jit(solution)/shard_map/ppermute | solution.py:22
  178.5 9.1 %collective-permute-start.5 = (f32[768,128]{0,1:T(8,128)S(1)}, f32[768,128]{0,1:T(8,128)S(1)}, u32[]{:S(2)}, u32[]{:S(2)}) collective-permute-start(f32[768,128]{0,1:T(8,128)S(1)} %get-tuple-element.27), channel_id=1, source_target_pairs={{1,0},{2,1},{3,2},{4,3},{5,4},{6,5},{7,6},{8,7},{9,8},{10,9},{11,1... | collective-permute-start | bytes 1179656 | tf_op jit(solution)/shard_map/ppermute | solution.py:23
  214.0 8.2 %collective-permute-start.6 = (f32[1024,128]{0,1:T(8,128)S(1)}, f32[1024,128]{0,1:T(8,128)S(1)}, u32[]{:S(2)}, u32[]{:S(2)}) collective-permute-start(f32[1024,128]{0,1:T(8,128)S(1)} %get-tuple-element.19), channel_id=1, source_target_pairs={{0,1},{1,2},{2,3},{3,4},{4,5},{5,6},{6,7},{7,8},{8,9},{9,10},{10,1... | collective-permute-start | bytes 1572872 | tf_op jit(solution)/shard_map/ppermute | solution.py:22
  216.0 10.5 %collective-permute-start.7 = (f32[1024,128]{0,1:T(8,128)S(1)}, f32[1024,128]{0,1:T(8,128)S(1)}, u32[]{:S(2)}, u32[]{:S(2)}) collective-permute-start(f32[1024,128]{0,1:T(8,128)S(1)} %get-tuple-element.20), channel_id=1, source_target_pairs={{1,0},{2,1},{3,2},{4,3},{5,4},{6,5},{7,6},{8,7},{9,8},{10,9},{11,1... | collective-permute-start | bytes 1572872 | tf_op jit(solution)/shard_map/ppermute | solution.py:23
  222.2 4.4 copy-start.9
  231.3 4.5 all-to-all-start.10
  236.4 24.9 %all-to-all-start.9 = ((f32[64,1,128]{2,1,0:T(1,128)}), f32[64,1,128]{2,1,0:T(1,128)S(1)}, u32[]{:S(2)}, u32[]{:S(2)}) async-start(f32[64,1,128]{2,1,0:T(1,128)} %broadcast_in_dim.81), calls=%async_computation.9 | async-start | bytes 65536 | tf_op jit(solution)/shard_map/all_to_all | solution.py:61
  261.9 13.0 %all-to-all-start.11 = ((f32[64,1,128]{2,1,0:T(1,128)}), f32[64,1,128]{2,1,0:T(1,128)S(1)}, u32[]{:S(2)}, u32[]{:S(2)}) async-start(f32[64,1,128]{2,1,0:T(1,128)} %broadcast_in_dim.83), calls=%async_computation.11 | async-start | bytes 65536 | tf_op jit(solution)/shard_map/all_to_all | solution.py:61
  276.4 0.8 copy-start.2
  278.2 39.9 %copy-start.3 = (f32[1024,128]{0,1:T(8,128)S(1)}, f32[1024,128]{0,1:T(8,128)}, u32[]{:S(2)}) copy-start(f32[1024,128]{0,1:T(8,128)} %copy-done.2) | copy-start | bytes 1572868
  335.8 8.6 %collective-permute-start.8 = (f32[768,128]{0,1:T(8,128)S(1)}, f32[768,128]{0,1:T(8,128)S(1)}, u32[]{:S(2)}, u32[]{:S(2)}) collective-permute-start(f32[768,128]{0,1:T(8,128)S(1)} %get-tuple-element.26), channel_id=1, source_target_pairs={{0,1},{1,2},{2,3},{3,4},{4,5},{5,6},{6,7},{7,8},{8,9},{9,10},{10,1... | collective-permute-start | bytes 1179656 | tf_op jit(solution)/shard_map/ppermute | solution.py:22
  339.7 9.1 %collective-permute-start.9 = (f32[768,128]{0,1:T(8,128)S(1)}, f32[768,128]{0,1:T(8,128)S(1)}, u32[]{:S(2)}, u32[]{:S(2)}) collective-permute-start(f32[768,128]{0,1:T(8,128)S(1)} %get-tuple-element.25), channel_id=1, source_target_pairs={{1,0},{2,1},{3,2},{4,3},{5,4},{6,5},{7,6},{8,7},{9,8},{10,9},{11,1... | collective-permute-start | bytes 1179656 | tf_op jit(solution)/shard_map/ppermute | solution.py:23
  378.4 8.0 %collective-permute-start.10 = (f32[1024,128]{0,1:T(8,128)S(1)}, f32[1024,128]{0,1:T(8,128)S(1)}, u32[]{:S(2)}, u32[]{:S(2)}) collective-permute-start(f32[1024,128]{0,1:T(8,128)S(1)} %get-tuple-element.17), channel_id=1, source_target_pairs={{0,1},{1,2},{2,3},{3,4},{4,5},{5,6},{6,7},{7,8},{8,9},{9,10},{10,1... | collective-permute-start | bytes 1572872 | tf_op jit(solution)/shard_map/ppermute | solution.py:22
  380.4 10.5 %collective-permute-start.11 = (f32[1024,128]{0,1:T(8,128)S(1)}, f32[1024,128]{0,1:T(8,128)S(1)}, u32[]{:S(2)}, u32[]{:S(2)}) collective-permute-start(f32[1024,128]{0,1:T(8,128)S(1)} %get-tuple-element.18), channel_id=1, source_target_pairs={{1,0},{2,1},{3,2},{4,3},{5,4},{6,5},{7,6},{8,7},{9,8},{10,9},{11,1... | collective-permute-start | bytes 1572872 | tf_op jit(solution)/shard_map/ppermute | solution.py:23
  386.5 34.6 %copy-start.6 = (f32[1024,128]{0,1:T(8,128)}, f32[1024,128]{0,1:T(8,128)S(1)}, u32[]{:S(2)}) copy-start(f32[1024,128]{0,1:T(8,128)S(1)} %collective-permute-done.10) | copy-start | bytes 1572868
  390.9 0.8 copy-start.8
  481.3 8.6 %collective-permute-start.12 = (f32[768,128]{0,1:T(8,128)S(1)}, f32[768,128]{0,1:T(8,128)S(1)}, u32[]{:S(2)}, u32[]{:S(2)}) collective-permute-start(f32[768,128]{0,1:T(8,128)S(1)} %get-tuple-element.24), channel_id=1, source_target_pairs={{0,1},{1,2},{2,3},{3,4},{4,5},{5,6},{6,7},{7,8},{8,9},{9,10},{10,1... | collective-permute-start | bytes 1179656 | tf_op jit(solution)/shard_map/ppermute | solution.py:22
  485.2 9.1 %collective-permute-start.13 = (f32[768,128]{0,1:T(8,128)S(1)}, f32[768,128]{0,1:T(8,128)S(1)}, u32[]{:S(2)}, u32[]{:S(2)}) collective-permute-start(f32[768,128]{0,1:T(8,128)S(1)} %get-tuple-element.23), channel_id=1, source_target_pairs={{1,0},{2,1},{3,2},{4,3},{5,4},{6,5},{7,6},{8,7},{9,8},{10,9},{11,1... | collective-permute-start | bytes 1179656 | tf_op jit(solution)/shard_map/ppermute | solution.py:23
  523.9 8.0 %collective-permute-start.14 = (f32[1024,128]{0,1:T(8,128)S(1)}, f32[1024,128]{0,1:T(8,128)S(1)}, u32[]{:S(2)}, u32[]{:S(2)}) collective-permute-start(f32[1024,128]{0,1:T(8,128)S(1)} %get-tuple-element.15), channel_id=1, source_target_pairs={{0,1},{1,2},{2,3},{3,4},{4,5},{5,6},{6,7},{7,8},{8,9},{9,10},{10,1... | collective-permute-start | bytes 1572872 | tf_op jit(solution)/shard_map/ppermute | solution.py:22
  525.9 10.5 %collective-permute-start.15 = (f32[1024,128]{0,1:T(8,128)S(1)}, f32[1024,128]{0,1:T(8,128)S(1)}, u32[]{:S(2)}, u32[]{:S(2)}) collective-permute-start(f32[1024,128]{0,1:T(8,128)S(1)} %get-tuple-element.16), channel_id=1, source_target_pairs={{1,0},{2,1},{3,2},{4,3},{5,4},{6,5},{7,6},{8,7},{9,8},{10,9},{11,1... | collective-permute-start | bytes 1572872 | tf_op jit(solution)/shard_map/ppermute | solution.py:23
  532.0 4.4 copy-start.5
  536.4 1.4 copy-start.7
  587.3 13.0 %all-to-all-start.30 = ((f32[64,1,128]{2,1,0:T(1,128)}), f32[64,1,128]{2,1,0:T(1,128)S(1)}, u32[]{:S(2)}, u32[]{:S(2)}) async-start(f32[64,1,128]{2,1,0:T(1,128)} %broadcast_in_dim.96), calls=%async_computation.30 | async-start | bytes 65536 | tf_op jit(solution)/shard_map/all_to_all | solution.py:61
  (1 other events, 0.8 us)
where the time goes:
time: 619 us; the launch traced here: 609 us
  blocking collectives  281 us (45%)
  matrix products  96.4 us (16%)
  waiting for transfers between devices  83.7 us (14%)
  starting transfers between devices  73.4 us (12%)
  local copies, waits for them, and re-layouts  39.1 us (6%)
  other arithmetic  32.4 us (5%)
    all_to_all x18, blocking collectives, sent_to_all(): return lax.all_to_all(copies, axis, split_axis=0, concat_axis=0, tiled=True)  178 us
    dot_general x4, matrix products, apply_local(): jnp.dot(schur_block, window, precision=HIGHEST, preferred_element_type=jn...  83.5 us
    all_to_all x5, blocking collectives, sum_in_two_steps(): return jnp.sum(lax.all_to_all(own, far, 0, 0, tiled=True), axis=0)  82.9 us
    ppermute x8, waiting for transfers between devices, extended_2(): lax.ppermute(initial, axis, [(b, a) for a, b in up])  35.2 us
    all_to_all x4, starting transfers between devices, sent_to_all(): return lax.all_to_all(copies, axis, split_axis=0, concat_axis=0, tiled=True)  29.4 us
    all_to_all x4, waiting for transfers between devices, sent_to_all(): return lax.all_to_all(copies, axis, split_axis=0, concat_axis=0, tiled=True)  24.7 us
    dynamic_update_slice x4, local copies, waits for them, and re-layouts, apply_local(): lax.dynamic_update_slice_in_dim(spread, product_block, start_row, 0)  23 us
    ppermute x8, waiting for transfers between devices, extended_2(): lax.ppermute(last, axis, up)  22.7 us
  transfers between devices with their start and end apart: 21, of which 21 were waited for; matrix products, arithmetic and copies ran while one was open for 0% of the time, Pallas kernels for 0%

commit v1 on v0

v1 whole, which is shorter than its diff:
```python
import functools

import jax
import jax.numpy as jnp
from jax import lax
from jax.experimental import pallas as pl
from jax.experimental.pallas import tpu as pltpu
from jax.sharding import Mesh
from jax.sharding import PartitionSpec as P


ITERS = 3
R = 128
AXES = ("gx", "gy_0", "gy_1", "gy_2")
MESH = pl.DeviceIdType.MESH
F32, BF16 = jnp.float32, jnp.bfloat16
HIGHEST = lax.Precision.HIGHEST
SLOTS = 4
N_AR = 2 + ITERS


def halves(x):
    high = x.astype(BF16)
    low = (x - high.astype(F32)).astype(BF16)
    return high, low


def wide(x):
    return jnp.concatenate(halves(x), axis=1)


def stacked(x):
    both = wide(x)
    return jnp.concatenate([both, both], axis=0)


def fold(acc):
    return acc[:, :R] + acc[:, R:]


def dot(a, b):
    return jnp.dot(a, b, preferred_element_type=F32)


def exact(a, b):
    return jnp.dot(a, b, precision=HIGHEST, preferred_element_type=F32)


def kernel(
    dims,
    slab,
    s_hbm,
    off_ref,
    rhs_hbm,
    b_hbm,
    load_ref,
    mult_ref,
    amp_ref,
    s_in,
    ss,
    b_own,
    r_own,
    hb,
    hr,
    ta,
    ha,
    wo,
    hw,
    e3,
    vv,
    y4,
    yy,
    rr,
    st,
    dd,
    bx,
    bto,
    btw,
    gm,
    mat1,
    cb1,
    own1,
    slot1,
    full1,
    mat2,
    cb2,
    own2,
    slot2,
    full2,
    in_sem,
    s_sem,
    ar_send,
    ar_recv,
    halo_send,
    halo_recv,
    a_send,
    a_recv,
    b_send,
    b_recv,
):
    nx, nz, ny, nc = dims
    count = nx * nz * ny * nc
    window = 2 * slab
    q = slab // 4
    half = R // 2 + 8
    x, z, y, c = (lax.axis_index(a) for a in AXES)
    me = ((x * nz + z) * ny + y) * nc + c
    first, last = me == 0, me == count - 1

    def place(line):
        return (
            line // (nz * ny * nc),
            (line // (ny * nc)) % nz,
            (line // nc) % ny,
            line % nc,
        )

    right = place((me + 1) % count)
    left = place((me + count - 1) % count)
    partner = (x, z, y, (c + 1) % nc)
    rings = {
        "y": [(x, z, (y + k) % ny, c) for k in range(1, ny)],
        "x": [((x + k) % nx, z, y, c) for k in range(1, nx)],
        "z": [(x, (z + k) % nz, y, c) for k in range(1, nz)],
    }
    peers = [left, right, partner] + rings["y"] + rings["x"] + rings["z"]

    def remote(src, dst, send, recv, device):
        return pltpu.make_async_remote_copy(
            src_ref=src, dst_ref=dst, send_sem=send, recv_sem=recv, device_id=device, device_id_type=MESH
        )

    pending = []

    def launch(copies):
        for copy in copies:
            copy.start()
        pending.extend(copies)

    class Reduction:
        def __init__(self, index, mat, cb, own, slot, full, rows):
            self.base = index * 11
            self.mat, self.cb, self.own, self.slot, self.full, self.rows = mat, cb, own, slot, full, rows
            self.order = ("y", "x", "z")
            self.step = 0
            self.flying = None

        def sems(self, k):
            return ar_send.at[self.base + k], ar_recv.at[self.base + k]

        def start(self):
            n = self.rows
            copy = remote(self.mat.at[pl.ds((1 - c) * n, n)], self.cb, *self.sems(0), partner)
            launch([copy])
            self.flying = [copy]

        def arrived(self):
            for copy in self.flying:
                copy.wait_recv()
            if self.step == 0:
                return self.mat[pl.ds(c * self.rows, self.rows), :] + self.cb[...]
            j = self.step - 1
            mine = self.own[j]
            got = [self.slot[j, k] for k in range(len(self.flying))]
            if len(got) == 1:
                return mine + got[0]
            return (mine + got[1]) + (got[0] + got[2])

        def ring(self):
            total = self.arrived()
            j = self.step
            self.own[j] = total
            copies = []
            for k, device in enumerate(rings[self.order[j]]):
                copies.append(remote(self.own.at[j], self.slot.at[j, k], *self.sems(1 + j * 3 + k), device))
            launch(copies)
            self.flying = copies
            self.step += 1

        def last(self):
            n = self.rows
            total = self.arrived()
            self.full[pl.ds(c * n, n), :] = total
            piece = self.full.at[pl.ds(c * n, n)]
            copy = remote(piece, piece, *self.sems(10), partner)
            launch([copy])
            self.flying = [copy]

        def result(self):
            self.flying[0].wait_recv()
            return self.full

    first_sum = Reduction(0, mat1, cb1, own1, slot1, full1, R)
    sums = [
        Reduction(1 + i, mat2.at[i], cb2.at[i], own2.at[i], slot2.at[i], full2.at[i], half)
        for i in range(1 + ITERS)
    ]

    def whole_halo(own, into, k):
        return [
            remote(own.at[pl.ds(q, 3 * q)], into.at[0, pl.ds(q, 3 * q)], halo_send.at[k], halo_recv.at[k], right),
            remote(own.at[pl.ds(0, 3 * q)], into.at[1, pl.ds(0, 3 * q)], halo_send.at[k + 1], halo_recv.at[k + 1], left),
        ]

    def to_right(i, k):
        rows, sem = pl.ds(k * q, q), 6 * i + k
        return remote(ta.at[i, 0, rows], ha.at[i, 0, rows], a_send.at[sem], a_recv.at[sem], right)

    def to_left(i, k):
        rows, sem = pl.ds(k * q, q), 6 * i + 2 + k
        return remote(ta.at[i, 1, rows], ha.at[i, 1, rows], a_send.at[sem], a_recv.at[sem], left)

    def image_right(i, k):
        rows, sem = pl.ds(k * q, q), 6 * i + k - 1
        return remote(wo.at[i, rows], hw.at[i, 0, rows], b_send.at[sem], b_recv.at[sem], right)

    def image_left(i, k):
        rows, sem = pl.ds(k * q, q), 6 * i + 3 + k
        return remote(wo.at[i, rows], hw.at[i, 1, rows], b_send.at[sem], b_recv.at[sem], left)

    b_in = pltpu.make_async_copy(b_hbm, b_own, in_sem.at[0])
    r_in = pltpu.make_async_copy(rhs_hbm, r_own, in_sem.at[1])
    b_in.start()
    r_in.start()
    strip = window // 8

    def strip_in(i):
        return pltpu.make_async_copy(s_hbm.at[0, pl.ds(i * strip, strip)], s_in.at[i % SLOTS], s_sem.at[i % SLOTS])

    for i in range(SLOTS):
        strip_in(i).start()
    barrier = pltpu.get_barrier_semaphore()
    for device in peers:
        pl.semaphore_signal(barrier, inc=1, device_id=device, device_id_type=MESH)

    off = off_ref[0]
    row_of = lax.broadcasted_iota(jnp.int32, (q, R), 0)

    def from_sides(lower, upper, k):
        lower = None if lower is None else jnp.where(first, 0.0, lower)
        upper = None if upper is None else jnp.where(last, 0.0, upper)
        if k == 0:
            return upper
        if k == 3:
            return lower
        return jnp.where(row_of + k * q < off, upper, lower)

    def halo_rows(ref, k):
        rows = pl.ds(k * q, q)
        lower = ref[0, rows, :] if k > 0 else None
        upper = ref[1, rows, :] if k < 3 else None
        return from_sides(lower, upper, k)

    def put_own(k, value):
        e3[slab + k * q : slab + (k + 1) * q, :] = value

    def put_halo(k, value):
        e3[k * q : (k + 1) * q, :] = value
        e3[2 * slab + k * q : 2 * slab + (k + 1) * q, :] = value

    b_in.wait()
    for k in range(4):
        rows = slice(k * q, (k + 1) * q)
        value = b_own[rows, :]
        high, low = halves(value)
        bx[rows, :R] = high
        bx[rows, R:] = low
        across = value.T
        high, low = halves(across)
        bto[:R, rows] = high
        bto[R:, rows] = low
        put_own(k, value)
    r_in.wait()
    pl.semaphore_wait(barrier, len(peers))
    b_halo = whole_halo(b_own, hb, 0)
    launch(b_halo)

    def quarters(acc):
        return (acc[:R, :R] + acc[R:, R:]) + (acc[:R, R:] + acc[R:, :R])

    mat1[:R, :] = quarters(dot(bto[...], bx[:slab, :]))
    mat1[R:, :] = quarters(dot(bto[...], wide(r_own[...])))
    first_sum.start()

    def split_strip(i):
        strip_in(i).wait()
        rows = pl.ds(i * strip, strip)
        high, low = halves(s_in[i % SLOTS])
        ss[rows, :window] = high
        ss[rows, window:] = low
        if i + SLOTS < 8:
            strip_in(i + SLOTS).start()

    for i in range(3):
        split_strip(i)
    first_sum.ring()
    r_halo = whole_halo(r_own, hr, 2)
    launch(r_halo)
    for i in range(3, 6):
        split_strip(i)
    first_sum.ring()
    for i in range(6, 8):
        split_strip(i)
    first_sum.ring()

    for copy in b_halo:
        copy.wait_recv()
    for k in range(4):
        value = halo_rows(hb, k)
        rows = slice(slab + k * q, slab + (k + 1) * q)
        high, low = halves(value)
        bx[rows, :R] = high
        bx[rows, R:] = low
        put_halo(k, value)

    block = window // 4

    def split_vector(basis):
        for i in range(8):
            rows = slice(i * strip, (i + 1) * strip)
            value = e3[pl.ds(off + i * strip, strip), :]
            high, low = halves(value)
            vv[rows, :R] = high
            vv[rows, R:] = low
            again = slice(window + i * strip, window + (i + 1) * strip)
            vv[again, :R] = high
            vv[again, R:] = low
            if basis:
                high, low = halves(value.T)
                btw[:R, rows] = high
                btw[R:, rows] = low

    def apply_block(i, total):
        start = pl.multiple_of(i * block, block)
        rows = pl.ds(start, block)
        product = fold(dot(ss[rows, :], vv[...]))
        y4[rows, :] = product
        high, low = halves(product)
        yy[rows, :R] = high
        yy[rows, R:] = low
        value = e3[pl.ds(off + start, block), :]
        return total + jnp.sum((value * product).reshape(block // 8, 8, R), axis=0)

    def apply_operator():
        total = lax.fori_loop(0, window // block, apply_block, jnp.zeros((8, R), F32))
        y4[window : window + slab, :] = y4[:slab, :]
        return quarters(dot(btw[...], yy[...])), total

    def send_buffers(i):
        for k in range(4):
            value = y4[pl.ds(window - off + k * q, q), :]
            below = row_of + k * q < off
            rows = slice(k * q, (k + 1) * q)
            if k < 3:
                ta[i, 0, rows, :] = jnp.where(below, value, 0.0)
            if k > 0:
                ta[i, 1, rows, :] = jnp.where(below, 0.0, value)

    def send_contributions(i):
        launch([to_right(i, 1), to_left(i, 1), to_right(i, 2), to_left(i, 2), to_right(i, 0), to_left(i, 3)])

    def own_image(i, k):
        rows = slice(k * q, (k + 1) * q)
        value = y4[pl.ds(slab - off + k * q, q), :]
        if k < 3:
            to_right(i, k).wait_recv()
            value = value + jnp.where(first, 0.0, ha[i, 0, rows, :])
        if k > 0:
            to_left(i, k).wait_recv()
            value = value + jnp.where(last, 0.0, ha[i, 1, rows, :])
        wo[i, rows, :] = value
        copies = []
        if k > 0:
            copies.append(image_right(i, k))
        if k < 3:
            copies.append(image_left(i, k))
        launch(copies)

    def halo_image(i, k):
        if k > 0:
            image_right(i, k).wait_recv()
        if k < 3:
            image_left(i, k).wait_recv()
        return halo_rows(hw.at[i], k)

    line = lax.broadcasted_iota(jnp.int32, (R, R), 0)
    lane = lax.broadcasted_iota(jnp.int32, (R, R), 1)

    def eliminate(begin, end):
        a = gm[...]
        for k in range(begin, end):
            inverse = 1.0 / a[k : k + 1, k : k + 1]
            pivot = jnp.where(lane[:1] == k, 1.0, a[k : k + 1, :]) * inverse
            column = a[:, k : k + 1]
            a = jnp.where(line == k, pivot, jnp.where(lane == k, 0.0, a) - column * pivot)
        gm[...] = a

    split_vector(True)
    coarse_image, _ = apply_operator()
    total = sums[0]
    mat2[0, :R, :] = coarse_image
    mat2[0, R:, :] = jnp.zeros((2 * half - R, R), F32)
    total.start()
    send_buffers(0)
    first_sum.last()
    total.ring()
    send_contributions(0)
    gm[...] = first_sum.result()[:R, :]
    eliminate(0, 32)
    total.ring()
    own_image(0, 1)
    eliminate(32, 48)
    own_image(0, 2)
    eliminate(48, 64)
    own_image(0, 0)
    own_image(0, 3)
    total.ring()
    eliminate(64, 96)
    total.last()
    eliminate(96, 128)
    gram_inverse = gm[...]
    start_load = exact(gram_inverse, load_ref[...])
    basis_image = total.result()[:R, :]
    coarse = full1[R:, :] - exact(basis_image, start_load)
    amp = exact(gram_inverse, coarse)
    for copy in r_halo:
        copy.wait_recv()

    def rows_sum(value):
        return jnp.sum(value.reshape(q // 8, 8, R), axis=0)

    start_wide, amp_wide = stacked(start_load), stacked(amp)
    energy_part = jnp.zeros((8, R), F32)
    for k in range(8):
        rows = slice(k * q, (k + 1) * q)
        if k < 4:
            image, known = wo[0, rows, :], r_own[rows, :]
            mult_ref[rows, :] = fold(dot(bx[rows, :], start_wide))
        else:
            image, known = halo_image(0, k - 4), halo_rows(hr, k - 4)
        residual = known - fold(dot(wide(image), start_wide))
        rr[rows, :] = residual
        projected = residual - fold(dot(bx[rows, :], amp_wide))
        if k < 4:
            put_own(k, projected)
            dd[rows, :] = projected
            energy_part = energy_part + rows_sum(projected * projected)
        else:
            put_halo(k - 4, projected)

    sub = lax.broadcasted_iota(jnp.int32, (8, R), 0)
    mixed_part = jnp.zeros((8, R), F32)
    energy_old = curvature = basis_old = None
    for it in range(ITERS):
        more = it < ITERS - 1
        slot = 1 + it
        total = sums[slot]
        split_vector(False)
        basis_part, curve_part = apply_operator()
        scalars = [jnp.sum(v, axis=0, keepdims=True) for v in (energy_part, curve_part, mixed_part)]
        mat2[slot, :R, :] = basis_part
        mat2[slot, R : R + 8, :] = jnp.where(
            sub == 0, scalars[0], jnp.where(sub == 1, scalars[1], jnp.where(sub == 2, scalars[2], 0.0))
        )
        mat2[slot, R + 8 :, :] = jnp.zeros((2 * half - R - 8, R), F32)
        total.start()
        if more:
            send_buffers(slot)
        total.ring()
        if more:
            send_contributions(slot)
        total.ring()
        if more:
            own_image(slot, 1)
            own_image(slot, 2)
        total.ring()
        if more:
            own_image(slot, 0)
            own_image(slot, 3)
        total.last()
        got = total.result()
        basis_image = got[:R, :]
        energy = got[R : R + 1, :]
        curve = got[R + 1 : R + 2, :]
        mixed = got[R + 2 : R + 3, :]
        if it == 0:
            beta = None
            curvature = curve
        else:
            beta = energy / energy_old
            curvature = curve + beta * (2.0 * mixed + beta * curvature)
            basis_image = basis_image + beta * basis_old
        step = energy / curvature
        energy_old, basis_old = energy, basis_image
        coarse = coarse - step * basis_image
        amp = exact(gram_inverse, coarse)
        if not more:
            amp_ref[...] = amp
        amp_wide = stacked(amp)
        energy_part = jnp.zeros((8, R), F32)
        mixed_part = jnp.zeros((8, R), F32)
        for k in range(8 if more else 4):
            rows = slice(k * q, (k + 1) * q)
            if k < 4:
                direction = dd[rows, :]
                if it > 0:
                    direction = e3[slab + k * q : slab + (k + 1) * q, :] + beta * direction
                    dd[rows, :] = direction
                mult_ref[rows, :] = mult_ref[rows, :] + step * direction
                if not more:
                    continue
                image = wo[slot, rows, :]
            else:
                image = halo_image(slot, k - 4)
            if it > 0:
                image = image + beta * st[rows, :]
            st[rows, :] = image
            residual = rr[rows, :] - step * image
            rr[rows, :] = residual
            projected = residual - fold(dot(bx[rows, :], amp_wide))
            if k < 4:
                put_own(k, projected)
                energy_part = energy_part + rows_sum(projected * projected)
                mixed_part = mixed_part + rows_sum(projected * image)
            else:
                put_halo(k - 4, projected)
    for copy in pending:
        copy.wait_send()


def local(dims, schur_blocks, offsets, right_side, coarse_basis, coarse_load):
    slab = right_side.shape[0]
    window = 2 * slab
    half = R // 2 + 8
    vmem, dma = pltpu.VMEM, pltpu.SemaphoreType.DMA
    anywhere = pl.BlockSpec(memory_space=pl.ANY)
    local_vmem = pl.BlockSpec(memory_space=pltpu.VMEM)
    return pl.pallas_call(
        functools.partial(kernel, dims, slab),
        out_shape=(
            jax.ShapeDtypeStruct((slab, R), F32),
            jax.ShapeDtypeStruct((R, R), F32),
        ),
        in_specs=[anywhere, pl.BlockSpec(memory_space=pltpu.SMEM), anywhere, anywhere, local_vmem],
        out_specs=(local_vmem, local_vmem),
        scratch_shapes=[
            vmem((SLOTS, window // 8, window), F32),
            vmem((window, 2 * window), BF16),
            vmem((slab, R), F32),
            vmem((slab, R), F32),
            vmem((2, slab, R), F32),
            vmem((2, slab, R), F32),
            vmem((ITERS, 2, slab, R), F32),
            vmem((ITERS, 2, slab, R), F32),
            vmem((ITERS, slab, R), F32),
            vmem((ITERS, 2, slab, R), F32),
            vmem((3 * slab, R), F32),
            vmem((2 * window, 2 * R), BF16),
            vmem((window + slab, R), F32),
            vmem((window, 2 * R), BF16),
            vmem((window, R), F32),
            vmem((window, R), F32),
            vmem((slab, R), F32),
            vmem((window, 2 * R), BF16),
            vmem((2 * R, slab), BF16),
            vmem((2 * R, window), BF16),
            vmem((R, R), F32),
            vmem((2 * R, R), F32),
            vmem((R, R), F32),
            vmem((3, R, R), F32),
            vmem((3, 3, R, R), F32),
            vmem((2 * R, R), F32),
            vmem((1 + ITERS, 2 * half, R), F32),
            vmem((1 + ITERS, half, R), F32),
            vmem((1 + ITERS, 3, half, R), F32),
            vmem((1 + ITERS, 3, 3, half, R), F32),
            vmem((1 + ITERS, 2 * half, R), F32),
            dma((2,)),
            dma((SLOTS,)),
            dma((11 * N_AR,)),
            dma((11 * N_AR,)),
            dma((4,)),
            dma((4,)),
            dma((6 * ITERS,)),
            dma((6 * ITERS,)),
            dma((6 * ITERS,)),
            dma((6 * ITERS,)),
        ],
        compiler_params=pltpu.CompilerParams(
            collective_id=0, has_side_effects=True, vmem_limit_bytes=67000000
        ),
    )(schur_blocks, offsets, right_side, coarse_basis, coarse_load)


def solution(mesh):
    if "gy_0" in mesh.shape:
        split = mesh
    else:
        split = Mesh(mesh.devices.reshape(mesh.shape["gx"], 4, 4, 2), AXES)
    dims = tuple(split.shape[a] for a in AXES)
    in_specs = (P(AXES, None, None), P(AXES), P(AXES, None), P(AXES, None), P())
    out_specs = (P(AXES, None), P())
    return jax.shard_map(
        functools.partial(local, dims), mesh=split, in_specs=in_specs, out_specs=out_specs, check_vma=False
    )
```

time: 619 us -> 138 us (0.22); the launches traced: 609 us -> 138 us
  blocking collectives: 281 us -> 0 us
  Pallas kernels: 0 us -> 133 us
  matrix products: 96.4 us -> 0 us
  waiting for transfers between devices: 83.7 us -> 0 us
  starting transfers between devices: 73.4 us -> 0 us
  local copies, waits for them, and re-layouts: 39.1 us -> 3.34 us
  other arithmetic: 32.4 us -> 0 us
    all_to_all x27 -> x0, blocking collectives: 281 us -> none  [the longest x18 178 us: sent_to_all(): return lax.all_to_all(copies, axis, split_axis=0, concat_axis=0, tiled=True)]
    pallas_call x0 -> x1, Pallas kernels: none -> 133 us  [local(): pl.pallas_call(functools.partial(kernel, dims, slab), out_shape=(jax.Shap...]
    dot_general x13 -> x0, matrix products: 93.4 us -> none  [the longest x4 83.5 us: apply_local(): jnp.dot(schur_block, window, precision=HIGHEST, preferred_element_type=jn...]
    ppermute x16 -> x0, waiting for transfers between devices: 57.9 us -> none  [the longest x8 35.2 us: extended_2(): lax.ppermute(initial, axis, [(b, a) for a, b in up])]
    ppermute x16 -> x0, starting transfers between devices: 39.3 us -> none  [the longest x8 20.5 us: extended_2(): lax.ppermute(last, axis, up)]
    all_to_all x5 -> x0, starting transfers between devices: 34.1 us -> none  [the longest x4 29.4 us: sent_to_all(): return lax.all_to_all(copies, axis, split_axis=0, concat_axis=0, tiled=True)]
    all_to_all x5 -> x0, waiting for transfers between devices: 25.8 us -> none  [the longest x4 24.7 us: sent_to_all(): return lax.all_to_all(copies, axis, split_axis=0, concat_axis=0, tiled=True)]
    dynamic_update_slice x4 -> x0, local copies, waits for them, and re-layouts: 23 us -> none  [apply_local(): lax.dynamic_update_slice_in_dim(spread, product_block, start_row, 0)]
  transfers between devices with their start and end apart: 21 -> 0, of which waited for: 21 -> 0; matrix products, arithmetic and copies ran while one was open for 0% -> 0% of each run, Pallas kernels for 0% -> 0%
where the time goes in v1:
time: 138 us
  Pallas kernels  133 us (96%)
  local copies, waits for them, and re-layouts  3.34 us (2%)
    pallas_call x1, Pallas kernels, local(): pl.pallas_call(functools.partial(kernel, dims, slab), out_shape=(jax.Shap...  133 us
    unnamed x2, local copies, waits for them, and re-layouts  3.34 us

profile of v1, /device:TPU:1, one launch (start us, length us, event | category | flops | bytes accessed | tf_op | source)
XLA Modules:
  0.0 137.5 jit_solution(15684491122069908406)
XLA Ops:
  1.3 132.9 %shard_map.68 = (f32[1024,128]{1,0:T(8,128)}, f32[128,128]{1,0:T(8,128)}) custom-call(f32[1,2048,2048]{2,1,0:T(8,128)} %s_hbm.1, s32[1]{0:T(128)S(6)} %copy.9.off_ref, f32[1024,128]{1,0:T(8,128)} %rhs_hbm.1, f32[1024,128]{1,0:T(8,128)} %b_hbm.1, f32[128,128]{1,0:T(8,128)} %load_ref.1), custom_call_target="tpu_custom_call" | custom-call | tf_op jit(solution)/shard_map/pallas_call | solution.py:538
  134.2 1.9 %copy.10 = f32[1024,128]{1,0:T(8,128)} copy(f32[1024,128]{1,0:T(8,128)} %get-tuple-element.4) | data formatting | bytes 1048576
  136.1 1.5 %copy.11 = f32[128,128]{1,0:T(8,128)} copy(f32[128,128]{1,0:T(8,128)} %get-tuple-element.5) | data formatting | bytes 131072
